TPU v7x, 16 devices: a 4x2x1 block of a 4x4x4 slice. The times are simulated.
16 devices in a mesh: dp: 4 (over y, z, core), tp: 4 (over x).
Axes of the slice: x: 4, y: 2, z: 1, core: 2. Of those that a mesh axis runs over, the one named last changes fastest.
The devices are a block of a 4x4x4 slice.
Arguments:
- x: bfloat16 [512, 12288], P('dp'), parts along dimension 0
- w_gate: bfloat16 [12288, 33792], P(None, 'tp')
- w_up: bfloat16 [12288, 33792], P(None, 'tp')
- w_down: bfloat16 [33792, 12288], P('tp')
Outputs:
- output: bfloat16 [512, 12288], P('dp'), parts along dimension 0
There are 4 independent parts. A program takes and returns all parts, laid end to end along the dimension named above; an argument that names none is the same for every part.
All inputs are finite; a program needn't handle non-finite values.
Results may differ from a plain program's by a relative error of at most 0.016.
Values are sent between devices in bfloat16 or wider.
A program may use at most 1.5 GiB of HBM per device.

v0:
```python
import jax
import jax.numpy as jnp
from jax import lax
from jax.sharding import PartitionSpec as P


def solution(mesh):
    def step(x, w_gate, w_up, w_down):
        gate = jnp.dot(x, w_gate, preferred_element_type=jnp.float32)
        up = jnp.dot(x, w_up, preferred_element_type=jnp.float32)
        hidden = (jax.nn.silu(gate) * up).astype(jnp.bfloat16)
        term = jnp.dot(hidden, w_down, preferred_element_type=jnp.float32).astype(jnp.bfloat16)
        return lax.psum(term, "tp")

    return jax.shard_map(
        step,
        mesh=mesh,
        in_specs=(P("dp", None), P(None, "tp"), P(None, "tp"), P("tp", None)),
        out_specs=P("dp", None),
        check_vma=False,
    )
```

profile of v0, /device:TPU:112, one launch (start us, length us, event | category | flops | bytes accessed | tf_op | source)
XLA Modules:
  0.0 288.8 jit_solution(15063131042663178935)
XLA Ops:
  6.5 0.0 copy-start
  6.6 0.0 all-reduce.2.cloned.1.call-start
  6.6 1.9 copy-done
  8.4 66.2 %fusion.1 = f32[128,8448]{1,0:T(8,128)} fusion(bf16[128,12288]{1,0:T(8,128)(2,1)S(1)} %copy-done, bf16[12288,8448]{1,0:T(8,128)(2,1)} %param.5), kind=kOutput, calls=%fused_computation.3 | convolution fusion | flops 26575110144 | bytes 215089152 | tf_op jit(solution)/shard_map/dot_general | solution.py:9
  74.6 66.8 %fusion = bf16[128,8448]{1,0:T(8,128)(2,1)} fusion(bf16[128,12288]{1,0:T(8,128)(2,1)S(1)} %copy-done, bf16[12288,8448]{1,0:T(8,128)(2,1)} %param.6, f32[128,8448]{1,0:T(8,128)} %fusion.1), kind=kOutput, calls=%fused_computation.2 | convolution fusion | flops 26581598208 | bytes 217251840 | tf_op jit(solution)/shard_map/dot_general | solution.py:10
  141.4 66.3 %convolution_convert_fusion = bf16[128,12288]{1,0:T(8,128)(2,1)} fusion(bf16[128,8448]{1,0:T(8,128)(2,1)} %fusion, bf16[8448,12288]{1,0:T(8,128)(2,1)} %param.7), kind=kOutput, calls=%fused_computation | convolution fusion | flops 26576683008 | bytes 212926464 | tf_op jit(solution)/shard_map/dot_general | solution.py:12
  207.7 0.1 all-reduce.2.cloned.1.call-update
  207.7 70.4 %all-reduce.2.cloned.1.call-done = bf16[128,12288]{1,0:T(8,128)(2,1)} async-done(((bf16[128,12288]{1,0:T(8,128)(2,1)}), bf16[128,12288]{1,0:T(8,128)(2,1)}) %all-reduce.2.cloned.1.call-update) | async-done | bytes 3145744 | tf_op jit(solution)/shard_map/psum | solution.py:13
  278.1 3.8 %copy.6 = bf16[128,12288]{1,0:T(8,128)(2,1)} copy(bf16[128,12288]{1,0:T(8,128)(2,1)} %all-reduce.2.cloned.1.call-done) | data formatting | bytes 6291456
Async XLA Ops:
  6.5 1.9 copy-start
  6.6 271.6 %all-reduce.2.cloned.1.call-start = ((), (), s32[]{:S(2)}) async-start(), calls=%async_computation | async-start | bytes 6291456 | tf_op jit(solution)/shard_map/psum | solution.py:13
Sparse Core Ops, SparseCore 0:
  207.8 70.2 all-reduce.1
where the time goes:
time: 289 us
  matrix products  199 us (69%)
  waiting for transfers between devices  70.4 us (24%)
  between operations  13.4 us (5%)
  local copies, waits for them, and re-layouts  5.72 us (2%)
    psum x1, waiting for transfers between devices, step(): return lax.psum(term, 'tp')  70.4 us
    dot_general x1, matrix products, step(): up = jnp.dot(x, w_up, preferred_element_type=jnp.float32)  66.8 us
    dot_general x1, matrix products, step(): jnp.dot(hidden, w_down, preferred_element_type=jnp.float32)  66.3 us
    dot_general x1, matrix products, step(): gate = jnp.dot(x, w_gate, preferred_element_type=jnp.float32)  66.2 us
  transfers between devices with their start and end apart: 1, of which 1 were waited for; matrix products, arithmetic and copies ran while one was open for 0% of the time, Pallas kernels for 0%

commit v1 on v0

v1 whole, which is shorter than its diff:
```python
import functools

import jax
import jax.numpy as jnp
from jax import lax
from jax.experimental import pallas as pl
from jax.experimental.pallas import tpu as pltpu
from jax.sharding import PartitionSpec as P

MESH = pl.DeviceIdType.MESH
SLOTS = 3
BN = 256
CN = 512
LAG_RS = 2
LAG_AG = 5
LAG_FW = 7
F32, BF16 = jnp.float32, jnp.bfloat16


def kernel(n, x_hbm, g_hbm, u_hbm, d_hbm, out, xb, hid, ring, accf, own, mid, s1_out, s1_in, s2_out, s2_in, fin,
           wsem, xsem, xsend, xrecv, hsend, hrecv, s1_send, s1_recv, s2_send, s2_recv, ag_send, near_recv, far_recv,
           sib_recv, fw_recv, fw_send):
    rows, depth = x_hbm.shape
    ff = d_hbm.shape[0]
    half = ff // 2
    full = half // BN
    rem = half - full * BN
    blocks = full + 1
    cols = out.shape[1] // 2
    chunks = cols // CN
    part = rows // n

    d, p = lax.axis_index("dp"), lax.axis_index("tp")
    c = lax.rem(d, 2)
    d0 = d - c
    sib = d0 + 1 - c
    right, left, opp = lax.rem(p + 1, n), lax.rem(p + n - 1, n), lax.rem(p + 2, n)
    fw_from = lax.rem(p + n - 1 + 2 * c, n)
    fw_to = lax.rem(p + n + 1 - 2 * c, n)

    def block_copies(b, first=False):
        s = 0 if first else lax.rem(b, SLOTS)
        w = rem if first else BN
        c0 = c * half if first else c * half + rem + (b - 1) * BN
        c0 = pl.multiple_of(c0, 128)
        return [
            pltpu.make_async_copy(h.at[:, pl.ds(c0, w)], ring.at[s, :, pl.ds(k * w, w)], wsem.at[s, k])
            for k, h in enumerate((g_hbm, u_hbm))
        ]

    def down_copy(t):
        s = lax.rem(t + blocks, SLOTS)
        c0 = pl.multiple_of(c * cols + t * CN, 128)
        return pltpu.make_async_copy(d_hbm.at[:, pl.ds(c0, CN)], ring.at[s, pl.ds(0, ff), :], wsem.at[s, 0])

    def start_block(b, first=False):
        for copy in block_copies(b, first):
            copy.start()

    def wait_block(b, first=False):
        for copy in block_copies(b, first):
            copy.wait()

    mine = pl.multiple_of(c * rows, rows)
    theirs = pl.multiple_of((1 - c) * rows, rows)
    x_copy = pltpu.make_async_copy(x_hbm, xb.at[pl.ds(mine, rows), :], xsem)
    x_copy.start()
    start_block(0, True)
    for b in range(1, SLOTS - 1):
        start_block(b)

    barrier = pltpu.get_barrier_semaphore()
    partners = [(sib, p)] + [(e, q) for e in (d, sib) for q in (left, right)]
    for dev in partners:
        pl.semaphore_signal(barrier, inc=1, device_id=dev, device_id_type=MESH)
    pl.semaphore_wait(barrier, len(partners))

    def remote(src, dst, send, recv, dev):
        return pltpu.make_async_remote_copy(
            src_ref=src, dst_ref=dst, send_sem=send, recv_sem=recv, device_id=dev, device_id_type=MESH)

    x_send = remote(x_hbm, xb.at[pl.ds(mine, rows), :], xsend, xrecv, (sib, p))
    x_send.start()
    x_copy.wait()
    remote(x_hbm, xb.at[pl.ds(theirs, rows), :], xsend, xrecv, (sib, p)).wait_recv()

    def act(r, w, c0):
        gate, up = r[:, :w], r[:, w:]
        hid[:, pl.ds(c0, w)] = (jax.nn.silu(gate) * up).astype(BF16)

    def send_hidden(c0, w):
        piece = hid.at[:, pl.ds(c0, w)]
        remote(piece, piece, hsend, hrecv, (sib, p)).start()

    def col(b):
        return pl.multiple_of(c * half + rem + (b - 1) * BN, 128)

    c_first = pl.multiple_of(c * half, 128)
    wait_block(0, True)
    start_block(SLOTS - 1)
    act(jnp.dot(xb[...], ring[0, :, : 2 * rem], preferred_element_type=F32), rem, c_first)

    def hidden_step(b, _):
        wait_block(b)
        ahead = b + SLOTS - 1

        @pl.when(ahead < blocks)
        def _():
            start_block(ahead)

        @pl.when(ahead >= blocks)
        def _():
            down_copy(ahead - blocks).start()

        @pl.when(b == 1)
        def _():
            send_hidden(c_first, rem)

        @pl.when(b > 1)
        def _():
            send_hidden(col(b - 1), BN)

        act(jnp.dot(xb[...], ring[lax.rem(b, SLOTS)], preferred_element_type=F32), BN, col(b))
        return 0

    lax.fori_loop(1, blocks, hidden_step, 0)

    own_half = pl.multiple_of(c * half, 128)
    sib_half = pl.multiple_of((1 - c) * half, 128)

    def stage(t):
        s1_out[t, 0] = accf[0, opp].astype(BF16)
        s1_out[t, 1] = accf[1, opp].astype(BF16)
        s2_out[t, 0, 1] = accf[1, right].astype(BF16)
        s2_out[t, 1, 0] = accf[0, left].astype(BF16)
        mid[t, 0] = accf[0, right]
        mid[t, 1] = accf[1, left]
        own[t, 0] = accf[0, p]
        own[t, 1] = accf[1, p]
        for g, q in ((0, right), (1, left)):
            remote(s1_out.at[t, g], s1_in.at[t, g], s1_send, s1_recv.at[t, g], (d, q)).start()

    def second_hop(t):
        for g, q in ((0, right), (1, left)):
            remote(s1_out.at[t, g], s1_in.at[t, g], s1_send, s1_recv.at[t, g], (d, q)).wait_recv()
            s2_out[t, g, g] = (mid[t, g] + s1_in[t, g].astype(F32)).astype(BF16)
        for g, q in ((0, right), (1, left)):
            remote(s2_out.at[t, g], s2_in.at[t, g], s2_send, s2_recv.at[t, g], (d, q)).start()

    def place(root, h, t):
        return out.at[pl.ds(pl.multiple_of(root * part, part), part), pl.ds(pl.multiple_of(h * cols + t * CN, 128), CN)]

    def finish(t):
        for g in (0, 1):
            remote(s2_out.at[t, g], s2_in.at[t, g], s2_send, s2_recv.at[t, g], (d, right)).wait_recv()
        for g in (0, 1):
            total = own[t, g] + s2_in[t, 0, g].astype(F32) + s2_in[t, 1, g].astype(F32)
            fin[t, g] = total.astype(BF16)
        for g in (0, 1):
            for q, ahead in ((right, g == 0), (left, g == 1)):
                sem = fw_recv.at[t, c] if ahead else near_recv
                remote(fin.at[t, g], place(p, c, t), ag_send, sem, (d0 + g, q)).start()
        remote(fin.at[t, 1 - c], place(p, c, t), ag_send, sib_recv, (sib, p)).start()
        r0 = pl.multiple_of(p * part, part)
        out[pl.ds(r0, part), pl.ds(pl.multiple_of(c * cols + t * CN, 128), CN)] = fin[t, c]

    def forward(t):
        for h in (0, 1):
            block = place(fw_from, h, t)
            remote(block, block, fw_send, fw_recv.at[t, h], (d, fw_to)).wait_recv()
            remote(block, block, fw_send, far_recv, (d, fw_to)).start()

    def behind(t):
        for lag, f in ((LAG_RS, second_hop), (LAG_AG, finish), (LAG_FW, forward)):
            @pl.when((t >= lag) & (t < chunks + lag))
            def _():
                f(t - lag)

    send_hidden(col(blocks - 1), BN)
    s0 = blocks % SLOTS
    down_copy(0).wait()
    down_copy(SLOTS - 1).start()
    r = jnp.dot(hid[:, pl.ds(own_half, half)], ring[s0, pl.ds(own_half, half), :], preferred_element_type=F32)
    accf[...] = r.reshape(accf.shape)
    theirs_h = hid.at[:, pl.ds(sib_half, half)]
    remote(theirs_h, theirs_h, hsend, hrecv, (sib, p)).wait_recv()
    r = jnp.dot(hid[:, pl.ds(sib_half, half)], ring[s0, pl.ds(sib_half, half), :], preferred_element_type=F32)
    accf[...] += r.reshape(accf.shape)
    stage(0)

    def down_step(t, _):
        down_copy(t).wait()

        @pl.when(t + SLOTS - 1 < chunks)
        def _():
            down_copy(t + SLOTS - 1).start()

        r = jnp.dot(hid[...], ring[lax.rem(t + blocks, SLOTS), pl.ds(0, ff), :], preferred_element_type=F32)
        accf[...] = r.reshape(accf.shape)
        stage(t)
        behind(t)
        return 0

    lax.fori_loop(1, chunks, down_step, 0)

    def drain_step(t, _):
        behind(t)
        return 0

    lax.fori_loop(chunks, chunks + LAG_FW, drain_step, 0)

    def row_block(q):
        return out.at[pl.ds(pl.multiple_of(q * part, part), part), :]

    near = row_block(fw_to)
    remote(near, near, ag_send, near_recv, (d, left)).wait_recv()
    far = row_block(opp)
    remote(far, far, ag_send, far_recv, (d, left)).wait_recv()
    sib_cols = out.at[pl.ds(pl.multiple_of(p * part, part), part), pl.ds(pl.multiple_of((1 - c) * cols, 128), cols)]
    remote(sib_cols, sib_cols, ag_send, sib_recv, (sib, p)).wait_recv()
    x_send.wait_send()
    mine_h = hid.at[:, pl.ds(own_half, half)]
    remote(mine_h, mine_h, hsend, hrecv, (sib, p)).wait_send()
    remote(s1_out, s1_in, s1_send, s1_recv.at[0, 0], (d, right)).wait_send()
    remote(s2_out, s2_in, s2_send, s2_recv.at[0, 0], (d, right)).wait_send()
    for _ in range(2):
        remote(fin, fin, ag_send, near_recv, (d, right)).wait_send()
    remote(sib_cols, sib_cols, ag_send, sib_recv, (sib, p)).wait_send()
    remote(near, near, fw_send, far_recv, (d, left)).wait_send()


def solution(mesh):
    n = mesh.shape["tp"]

    def step(x, w_gate, w_up, w_down):
        rows, depth = x.shape
        ff, width = w_down.shape
        cols, part = width // 2, rows // n
        chunks = cols // CN
        dma = pltpu.SemaphoreType.DMA
        flops = 2 * rows * (2 * depth * ff + ff * width)
        return pl.pallas_call(
            functools.partial(kernel, n),
            out_shape=jax.ShapeDtypeStruct((rows, width), BF16),
            in_specs=[pl.BlockSpec(memory_space=pl.ANY)] * 4,
            out_specs=pl.BlockSpec(memory_space=pltpu.VMEM),
            scratch_shapes=[
                pltpu.VMEM((2 * rows, depth), BF16),
                pltpu.VMEM((2 * rows, ff), BF16),
                pltpu.VMEM((SLOTS, depth, 2 * BN), BF16),
                pltpu.VMEM((2, n, part, CN), F32),
                pltpu.VMEM((chunks, 2, part, CN), F32),
                pltpu.VMEM((chunks, 2, part, CN), F32),
                pltpu.VMEM((chunks, 2, part, CN), BF16),
                pltpu.VMEM((chunks, 2, part, CN), BF16),
                pltpu.VMEM((chunks, 2, 2, part, CN), BF16),
                pltpu.VMEM((chunks, 2, 2, part, CN), BF16),
                pltpu.VMEM((chunks, 2, part, CN), BF16),
                dma((SLOTS, 2)), dma, dma, dma, dma, dma,
                dma, dma((chunks, 2)), dma, dma((chunks, 2)),
                dma, dma, dma, dma, dma((chunks, 2)), dma,
            ],
            compiler_params=pltpu.CompilerParams(
                collective_id=0, has_side_effects=True, vmem_limit_bytes=67043328),
            cost_estimate=pl.CostEstimate(
                flops=flops, bytes_accessed=3 * depth * ff, transcendentals=rows * ff),
        )(x, w_gate, w_up, w_down)

    return jax.shard_map(
        step,
        mesh=mesh,
        in_specs=(P("dp", None), P(None, "tp"), P(None, "tp"), P("tp", None)),
        out_specs=P("dp", None),
        check_vma=False,
    )
```

time: 289 us -> 136 us (0.47)
  matrix products: 199 us -> 0 us
  Pallas kernels: 0 us -> 132 us
  waiting for transfers between devices: 70.4 us -> 0 us
  between operations: 13.4 us -> 0.01 us
    dot_general x3 -> x0, matrix products: 199 us -> none  [the longest x1 66.8 us: step(): up = jnp.dot(x, w_up, preferred_element_type=jnp.float32)]
    pallas_call x0 -> x1, Pallas kernels: none -> 132 us  [step(): pl.pallas_call(functools.partial(kernel, n), out_shape=jax.ShapeDtypeStru...]
    psum x1 -> x0, waiting for transfers between devices: 70.4 us -> none  [step(): return lax.psum(term, 'tp')]
  transfers between devices with their start and end apart: 1 -> 0, of which waited for: 1 -> 0; matrix products, arithmetic and copies ran while one was open for 0% -> 0% of each run, Pallas kernels for 0% -> 0%
where the time goes in v1:
time: 136 us
  Pallas kernels  132 us (97%)
  local copies, waits for them, and re-layouts  3.83 us (3%)
    pallas_call x1, Pallas kernels, step(): pl.pallas_call(functools.partial(kernel, n), out_shape=jax.ShapeDtypeStru...  132 us
    unnamed x1, local copies, waits for them, and re-layouts  3.83 us

profile of v1, /device:TPU:112, one launch (start us, length us, event | category | flops | bytes accessed | tf_op | source)
XLA Modules:
  0.0 136.3 jit_solution(959669534441411294)
XLA Ops:
  0.0 132.5 %shard_map.46 = bf16[128,12288]{1,0:T(8,128)(2,1)} custom-call(bf16[128,12288]{1,0:T(8,128)(2,1)} %x_hbm.1, bf16[12288,8448]{1,0:T(8,128)(2,1)} %g_hbm.1, bf16[12288,8448]{1,0:T(8,128)(2,1)} %u_hbm.1, bf16[8448,12288]{1,0:T(8,128)(2,1)} %d_hbm.1), custom_call_target="tpu_custom_call" | custom-call | flops 79725330432 | bytes 311427072 | tf_op jit(solution)/shard_map/pallas_call | solution.py:242
  132.5 3.8 %copy.6 = bf16[128,12288]{1,0:T(8,128)(2,1)} copy(bf16[128,12288]{1,0:T(8,128)(2,1)} %shard_map.46) | data formatting | bytes 6291456

commit v2 on v1

--- a/solution.py
+++ b/solution.py
@@ -11,9 +11,9 @@
 SLOTS = 3
 BN = 256
 CN = 512
-LAG_RS = 2
-LAG_AG = 5
-LAG_FW = 7
+LAG_RS = 1
+LAG_AG = 3
+LAG_FW = 5
 F32, BF16 = jnp.float32, jnp.bfloat16
 
 
@@ -241,7 +241,7 @@
         flops = 2 * rows * (2 * depth * ff + ff * width)
         return pl.pallas_call(
             functools.partial(kernel, n),
-            out_shape=jax.ShapeDtypeStruct((rows, width), BF16),
+            out_shape=pltpu.VMEM((rows, width), BF16),
             in_specs=[pl.BlockSpec(memory_space=pl.ANY)] * 4,
             out_specs=pl.BlockSpec(memory_space=pltpu.VMEM),
             scratch_shapes=[
@@ -261,7 +261,7 @@
                 dma, dma, dma, dma, dma((chunks, 2)), dma,
             ],
             compiler_params=pltpu.CompilerParams(
-                collective_id=0, has_side_effects=True, vmem_limit_bytes=67043328),
+                collective_id=0, has_side_effects=True, vmem_limit_bytes=63700000),
             cost_estimate=pl.CostEstimate(
                 flops=flops, bytes_accessed=3 * depth * ff, transcendentals=rows * ff),
         )(x, w_gate, w_up, w_down)

time: 136 us -> 130 us (0.956)
  Pallas kernels: 132 us -> 129 us
  local copies, waits for them, and re-layouts: 3.83 us -> 1.67 us
    pallas_call x1, Pallas kernels: 132 us -> 129 us  [step(): pl.pallas_call(functools.partial(kernel, n), out_shape=pltpu.VMEM((rows,...]
    unnamed x1, local copies, waits for them, and re-layouts: 3.83 us -> 1.67 us
where the time goes in v2:
time: 130 us
  Pallas kernels  129 us (99%)
  local copies, waits for them, and re-layouts  1.67 us (1%)
    pallas_call x1, Pallas kernels, step(): pl.pallas_call(functools.partial(kernel, n), out_shape=pltpu.VMEM((rows,...  129 us

profile of v2, /device:TPU:112, one launch (start us, length us, event | category | flops | bytes accessed | tf_op | source)
XLA Modules:
  0.0 130.3 jit_solution(15834406668038460054)
XLA Ops:
  0.0 128.6 %shard_map.46 = bf16[128,12288]{1,0:T(8,128)(2,1)S(1)} custom-call(bf16[128,12288]{1,0:T(8,128)(2,1)} %x_hbm.1, bf16[12288,8448]{1,0:T(8,128)(2,1)} %g_hbm.1, bf16[12288,8448]{1,0:T(8,128)(2,1)} %u_hbm.1, bf16[8448,12288]{1,0:T(8,128)(2,1)} %d_hbm.1), custom_call_target="tpu_custom_call" | custom-call | flops 79725330432 | bytes 311427072 | tf_op jit(solution)/shard_map/pallas_call | solution.py:242
  128.6 1.7 %copy.6 = bf16[128,12288]{1,0:T(8,128)(2,1)} copy(bf16[128,12288]{1,0:T(8,128)(2,1)S(1)} %shard_map.46) | data formatting | bytes 6291456

commit v3 on v2

--- a/solution.py
+++ b/solution.py
@@ -10,10 +10,11 @@
 MESH = pl.DeviceIdType.MESH
 SLOTS = 3
 BN = 256
+XP = 4
 CN = 512
 LAG_RS = 1
 LAG_AG = 3
-LAG_FW = 5
+LAG_FW = 6
 F32, BF16 = jnp.float32, jnp.bfloat16
 
 
@@ -63,8 +64,14 @@
 
     mine = pl.multiple_of(c * rows, rows)
     theirs = pl.multiple_of((1 - c) * rows, rows)
-    x_copy = pltpu.make_async_copy(x_hbm, xb.at[pl.ds(mine, rows), :], xsem)
-    x_copy.start()
+    cut = depth // XP
+
+    def x_copy(i):
+        piece = pl.ds(i * cut, cut)
+        return pltpu.make_async_copy(x_hbm.at[:, piece], xb.at[pl.ds(mine, rows), piece], xsem.at[i])
+
+    for i in range(XP):
+        x_copy(i).start()
     start_block(0, True)
     for b in range(1, SLOTS - 1):
         start_block(b)
@@ -79,10 +86,13 @@
         return pltpu.make_async_remote_copy(
             src_ref=src, dst_ref=dst, send_sem=send, recv_sem=recv, device_id=dev, device_id_type=MESH)
 
-    x_send = remote(x_hbm, xb.at[pl.ds(mine, rows), :], xsend, xrecv, (sib, p))
-    x_send.start()
-    x_copy.wait()
-    remote(x_hbm, xb.at[pl.ds(theirs, rows), :], xsend, xrecv, (sib, p)).wait_recv()
+    def x_send(i, base):
+        piece = xb.at[pl.ds(base, rows), pl.ds(i * cut, cut)]
+        return remote(piece, piece, xsend.at[i], xrecv.at[i], (sib, p))
+
+    for i in range(XP):
+        x_copy(i).wait()
+        x_send(i, mine).start()
 
     def act(r, w, c0):
         gate, up = r[:, :w], r[:, w:]
@@ -98,7 +108,12 @@
     c_first = pl.multiple_of(c * half, 128)
     wait_block(0, True)
     start_block(SLOTS - 1)
-    act(jnp.dot(xb[...], ring[0, :, : 2 * rem], preferred_element_type=F32), rem, c_first)
+    total = jnp.zeros((2 * rows, 2 * rem), F32)
+    for i in range(XP):
+        x_send(i, theirs).wait_recv()
+        piece = slice(i * cut, (i + 1) * cut)
+        total += jnp.dot(xb[:, piece], ring[0, piece, : 2 * rem], preferred_element_type=F32)
+    act(total, rem, c_first)
 
     def hidden_step(b, _):
         wait_block(b)
@@ -156,10 +171,10 @@
         for g in (0, 1):
             total = own[t, g] + s2_in[t, 0, g].astype(F32) + s2_in[t, 1, g].astype(F32)
             fin[t, g] = total.astype(BF16)
-        for g in (0, 1):
-            for q, ahead in ((right, g == 0), (left, g == 1)):
-                sem = fw_recv.at[t, c] if ahead else near_recv
-                remote(fin.at[t, g], place(p, c, t), ag_send, sem, (d0 + g, q)).start()
+        for g, q in ((0, right), (1, left)):
+            remote(fin.at[t, g], place(p, c, t), ag_send, fw_recv.at[t, c], (d0 + g, q)).start()
+        for g, q in ((1, right), (0, left)):
+            remote(fin.at[t, g], place(p, c, t), ag_send, near_recv, (d0 + g, q)).start()
         remote(fin.at[t, 1 - c], place(p, c, t), ag_send, sib_recv, (sib, p)).start()
         r0 = pl.multiple_of(p * part, part)
         out[pl.ds(r0, part), pl.ds(pl.multiple_of(c * cols + t * CN, 128), CN)] = fin[t, c]
@@ -218,7 +233,8 @@
     remote(far, far, ag_send, far_recv, (d, left)).wait_recv()
     sib_cols = out.at[pl.ds(pl.multiple_of(p * part, part), part), pl.ds(pl.multiple_of((1 - c) * cols, 128), cols)]
     remote(sib_cols, sib_cols, ag_send, sib_recv, (sib, p)).wait_recv()
-    x_send.wait_send()
+    for i in range(XP):
+        x_send(i, mine).wait_send()
     mine_h = hid.at[:, pl.ds(own_half, half)]
     remote(mine_h, mine_h, hsend, hrecv, (sib, p)).wait_send()
     remote(s1_out, s1_in, s1_send, s1_recv.at[0, 0], (d, right)).wait_send()
@@ -256,7 +272,7 @@
                 pltpu.VMEM((chunks, 2, 2, part, CN), BF16),
                 pltpu.VMEM((chunks, 2, 2, part, CN), BF16),
                 pltpu.VMEM((chunks, 2, part, CN), BF16),
-                dma((SLOTS, 2)), dma, dma, dma, dma, dma,
+                dma((SLOTS, 2)), dma((XP,)), dma((XP,)), dma((XP,)), dma, dma,
                 dma, dma((chunks, 2)), dma, dma((chunks, 2)),
                 dma, dma, dma, dma, dma((chunks, 2)), dma,
             ],

time: 130 us -> 129 us (level)
  Pallas kernels: 129 us -> 127 us
    pallas_call x1, Pallas kernels: 129 us -> 127 us  [step(): pl.pallas_call(functools.partial(kernel, n), out_shape=pltpu.VMEM((rows,...]
where the time goes in v3:
time: 129 us
  Pallas kernels  127 us (98%)
  local copies, waits for them, and re-layouts  1.67 us (1%)
    pallas_call x1, Pallas kernels, step(): pl.pallas_call(functools.partial(kernel, n), out_shape=pltpu.VMEM((rows,...  127 us

profile of v3, /device:TPU:112, one launch (start us, length us, event | category | flops | bytes accessed | tf_op | source)
XLA Modules:
  0.0 128.9 jit_solution(12893010354290234979)
XLA Ops:
  0.0 127.3 %shard_map.46 = bf16[128,12288]{1,0:T(8,128)(2,1)S(1)} custom-call(bf16[128,12288]{1,0:T(8,128)(2,1)} %x_hbm.1, bf16[12288,8448]{1,0:T(8,128)(2,1)} %g_hbm.1, bf16[12288,8448]{1,0:T(8,128)(2,1)} %u_hbm.1, bf16[8448,12288]{1,0:T(8,128)(2,1)} %d_hbm.1), custom_call_target="tpu_custom_call" | custom-call | flops 79725330432 | bytes 311427072 | tf_op jit(solution)/shard_map/pallas_call | solution.py:258
  127.3 1.7 %copy.6 = bf16[128,12288]{1,0:T(8,128)(2,1)} copy(bf16[128,12288]{1,0:T(8,128)(2,1)S(1)} %shard_map.46) | data formatting | bytes 6291456
